TPU v7x, 32 devices: a whole 2x2x4 slice. The times are simulated.
32 devices in a mesh: gz: 16 (over z, x, core), gy: 2 (over y).
Axes of the slice: x: 2, y: 2, z: 4, core: 2. Of those that a mesh axis runs over, the one named last changes fastest.
Arguments:
- spread_weights: float32 [64, 32768], P(None, ('gz', 'gy')), may hold values from -6 to 6
- spread_base: int32 [3, 32768], P(None, ('gz', 'gy')), may hold values from 0 to 383, as said below
- qm_base: int32 [3, 4096], P(None, ('gz', 'gy')), may hold values from 0 to 383, as said below
- qm_frac: float32 [3, 4096], P(None, ('gz', 'gy')), may hold values from 0 to 1
- qm_charge: float32 [4096], P(('gz', 'gy')), may hold values from -3 to 3
Outputs:
- qm_forces: float32 [3, 4096], P(None, ('gz', 'gy'))
Inputs may be any that keep to these rules, and one draw needn't show every extreme that they name: For point charge j let d = j // 1024, p = d // 2 and q = d % 2; then spread_base[0, j] lies in [p * 24, (p + 1) * 24) and spread_base[1, j] in [q * 192, (q + 1) * 192); spread_base[2, j] is any cell. For quantum-region atom i let d = i // 128, p = d // 2 and q = d % 2; then qm_base[0, i] lies in [p * 24, (p + 1) * 24) and qm_base[1, i] in [q * 192, (q + 1) * 192); qm_base[2, i] is any cell.
All inputs are finite; a program needn't handle non-finite values.
Results may differ from a plain program's by a relative error of at most 0.0003.
Values sent between devices are 32-bit elements; how exact they have to be, the bound alone decides.
No kernel may reach another device: no remote copies, remote signals or barrier semaphores. Data moves between devices by JAX's collectives and lax.ppermute only.
A program may use at most 256 MiB of HBM per device.

v0:
```python
import math

import jax
import jax.numpy as jnp
from jax import lax
from jax.sharding import PartitionSpec as P

GRID = 384
ORDER = 4


SPLITTING = 0.8
HIGHEST = lax.Precision.HIGHEST


def passed_along(block, axis, distance):
    devices = range(lax.axis_size(axis))
    route = [((i - distance) % len(devices), i) for i in devices]
    return lax.ppermute(block, axis, route)


def moduli(index, points):
    signed = jnp.where(index < points // 2, index, index - points).astype(jnp.float32) / points
    spline = 2.0 / 3.0 + jnp.cos(2.0 * math.pi / points * index.astype(jnp.float32)) / 3.0
    return (signed * signed, 1.0 / (spline * spline), index == points // 2)


def influence(first, second, third, points):
    sq_one, mod_one, edge_one = moduli(first, points)
    sq_two, mod_two, edge_two = moduli(second, points)
    sq_three, mod_three, edge_three = moduli(third, points)
    total = sq_one + sq_two + sq_three
    safe = jnp.where(total > 0.0, total, 1.0)
    value = (
        mod_one
        * mod_two
        * mod_three
        * jnp.exp(-(math.pi * math.pi / (SPLITTING * SPLITTING)) * total)
        / (math.pi * safe)
    )
    keep = (total > 0.0) & jnp.logical_not(edge_one | edge_two | edge_three)
    return jnp.where(keep, value, 0.0)


def spline_weights(frac):
    remain = 1.0 - frac
    square = frac * frac
    cubed = square * frac
    values = jnp.stack(
        [
            remain * remain * remain / 6.0,
            (3.0 * cubed - 6.0 * square + 4.0) / 6.0,
            (-3.0 * cubed + 3.0 * square + 3.0 * frac + 1.0) / 6.0,
            cubed / 6.0,
        ]
    )
    slopes = jnp.stack(
        [
            -0.5 * remain * remain,
            (3.0 * square - 4.0 * frac) / 2.0,
            (-3.0 * square + 2.0 * frac + 1.0) / 2.0,
            0.5 * square,
        ]
    )
    return (values, slopes)


def angle_tables(rows_in, cols_in, points):
    product = rows_in[:, None] * cols_in[None, :] % points
    angle = 2.0 * math.pi / points * product.astype(jnp.float32)
    return (jnp.cos(angle), jnp.sin(angle))


def transform(real_part, imag_part, form, cosine, sine, sign):
    first = jnp.einsum(form, real_part, cosine, precision=HIGHEST)
    second = jnp.einsum(form, imag_part, sine, precision=HIGHEST)
    third = jnp.einsum(form, imag_part, cosine, precision=HIGHEST)
    fourth = jnp.einsum(form, real_part, sine, precision=HIGHEST)
    return (first - sign * second, third + sign * fourth)


def spread_grid(spread_weights, spread_base, z_first, y_first, z_extent, y_extent, points):
    count = spread_weights.shape[1]
    weights = spread_weights.reshape(ORDER, ORDER, ORDER, count)
    shifts = jnp.arange(ORDER, dtype=jnp.int32)
    local_z = spread_base[0] - z_first
    local_y = spread_base[1] - y_first
    plane_hits = (
        jnp.arange(z_extent, dtype=jnp.int32)[None, :, None]
        == local_z[None, None, :] + shifts[:, None, None]
    ).astype(jnp.float32)
    row_hits = (
        jnp.arange(y_extent, dtype=jnp.int32)[None, :, None]
        == local_y[None, None, :] + shifts[:, None, None]
    ).astype(jnp.float32)
    column_cells = (spread_base[2][None, :] + shifts[:, None]) % points
    column_hits = (
        jnp.arange(points, dtype=jnp.int32)[None, None, :] == column_cells[:, :, None]
    ).astype(jnp.float32)
    by_plane = jnp.sum(plane_hits[:, None, :, None, :] * weights[:, :, None, :, :], axis=0)
    placed = jnp.sum(by_plane[:, :, None, :, :] * row_hits[:, None, :, None, :], axis=0)
    charge = jnp.dot(
        placed.reshape(z_extent * y_extent, ORDER * count),
        column_hits.reshape(ORDER * count, points),
        precision=HIGHEST,
        preferred_element_type=jnp.float32,
    )
    return charge.reshape(z_extent, y_extent, points)


def line_tables(cells, values, slopes, extent):
    hits = (jnp.arange(extent, dtype=jnp.int32)[None, :, None] == cells[:, None, :]).astype(
        jnp.float32
    )
    return (jnp.sum(hits * values[:, None, :], axis=0), jnp.sum(hits * slopes[:, None, :], axis=0))


def interpolate(potential, qm_base, qm_frac, qm_charge, z_first, y_first):
    z_extent, y_extent, points = potential.shape
    count = qm_charge.shape[0]
    shifts = jnp.arange(ORDER, dtype=jnp.int32)[:, None]
    w_z, d_z = spline_weights(qm_frac[0])
    w_y, d_y = spline_weights(qm_frac[1])
    w_x, d_x = spline_weights(qm_frac[2])
    plane_w, plane_d = line_tables(qm_base[0][None, :] - z_first + shifts, w_z, d_z, z_extent)
    row_w, row_d = line_tables(qm_base[1][None, :] - y_first + shifts, w_y, d_y, y_extent)
    column_w, column_d = line_tables((qm_base[2][None, :] + shifts) % points, w_x, d_x, points)
    along_x = jnp.dot(
        potential.reshape(z_extent * y_extent, points),
        jnp.concatenate([column_w, column_d], axis=1),
        precision=HIGHEST,
        preferred_element_type=jnp.float32,
    ).reshape(z_extent, y_extent, 2, count)
    plain = along_x[:, :, 0, :]
    sloped = along_x[:, :, 1, :]
    force_z = jnp.sum(plain * plane_d[:, None, :] * row_w[None, :, :], axis=(0, 1))
    force_y = jnp.sum(plain * plane_w[:, None, :] * row_d[None, :, :], axis=(0, 1))
    force_x = jnp.sum(sloped * plane_w[:, None, :] * row_w[None, :, :], axis=(0, 1))
    return jnp.stack([-qm_charge * force_z, -qm_charge * force_y, -qm_charge * force_x])


def shards(spread_weights, spread_base, qm_base, qm_frac, qm_charge):
    points = GRID
    margin = ORDER - 1
    count_z = lax.axis_size("gz")
    count_y = lax.axis_size("gy")
    z_local = points // count_z
    y_local = points // count_y
    z_extent = z_local + margin
    y_extent = y_local + margin
    z_first = lax.axis_index("gz") * z_local
    y_first = lax.axis_index("gy") * y_local
    charge = spread_grid(spread_weights, spread_base, z_first, y_first, z_extent, y_extent, points)
    spill_rows = passed_along(charge[:, y_local:, :], "gy", 1)
    charge = charge[:, :y_local, :].at[:, :margin, :].add(spill_rows)
    spill_planes = passed_along(charge[z_local:], "gz", 1)
    charge = charge[:z_local].at[:margin].add(spill_planes)
    kx_count = points // 2
    kx_weight = jnp.where(jnp.arange(kx_count, dtype=jnp.int32) == 0, 1.0, 2.0).astype(jnp.float32)
    positions = jnp.arange(points, dtype=jnp.int32)
    cos_x, sin_x = angle_tables(positions, jnp.arange(kx_count, dtype=jnp.int32), points)
    real_x = jnp.einsum("zyx,xk->kyz", charge, cos_x, precision=HIGHEST)
    imag_x = -jnp.einsum("zyx,xk->kyz", charge, sin_x, precision=HIGHEST)
    packed = jnp.stack([real_x, imag_x]).reshape(2, kx_count, y_local * z_local)
    moved = lax.all_to_all(packed, "gy", split_axis=1, concat_axis=2, tiled=True)
    kx_local = kx_count // count_y
    lines = moved.reshape(2, kx_local, count_y, y_local, z_local)
    lines = lines.reshape(2, kx_local, points, z_local)
    cos_full, sin_full = angle_tables(positions, positions, points)
    real_y, imag_y = transform(lines[0], lines[1], "xyz,yk->kzx", cos_full, sin_full, -1.0)
    packed = jnp.stack([real_y, imag_y]).reshape(2, points, z_local * kx_local)
    moved = lax.all_to_all(packed, "gz", split_axis=1, concat_axis=2, tiled=True)
    ky_local = points // count_z
    lines = moved.reshape(2, ky_local, count_z, z_local, kx_local)
    lines = lines.reshape(2, ky_local, points, kx_local)
    real_z, imag_z = transform(lines[0], lines[1], "yzx,zk->yxk", cos_full, sin_full, -1.0)
    ky_index = lax.axis_index("gz") * ky_local + jnp.arange(ky_local, dtype=jnp.int32)
    kx_index = lax.axis_index("gy") * kx_local + jnp.arange(kx_local, dtype=jnp.int32)
    green = influence(
        positions[None, None, :], ky_index[:, None, None], kx_index[None, :, None], points
    )
    real_z = real_z * green
    imag_z = imag_z * green
    z_rows = (
        (
            jnp.arange(count_z, dtype=jnp.int32)[:, None] * z_local
            + jnp.arange(z_local, dtype=jnp.int32)[None, :]
        )
        % points
    ).reshape(-1)
    cos_z, sin_z = angle_tables(positions, z_rows, points)
    back_real, back_imag = transform(real_z, imag_z, "yxk,kp->pyx", cos_z, sin_z, 1.0)
    packed = jnp.stack([back_real, back_imag]).reshape(2, count_z * z_local, ky_local * kx_local)
    moved = lax.all_to_all(packed, "gz", split_axis=1, concat_axis=2, tiled=True).reshape(
        2, z_local, points, kx_local
    )
    y_rows = (
        (
            jnp.arange(count_y, dtype=jnp.int32)[:, None] * y_local
            + jnp.arange(y_local, dtype=jnp.int32)[None, :]
        )
        % points
    ).reshape(-1)
    cos_y, sin_y = angle_tables(positions, y_rows, points)
    back_real, back_imag = transform(moved[0], moved[1], "zkx,kp->pxz", cos_y, sin_y, 1.0)
    packed = jnp.stack([back_real, back_imag]).reshape(2, count_y * y_local, kx_local * z_local)
    moved = lax.all_to_all(packed, "gy", split_axis=1, concat_axis=2, tiled=True).reshape(
        2, y_local, kx_count, z_local
    )
    scale = 1.0 / float(points * points * points)
    potential = (
        jnp.einsum("ykz,xk->zyx", moved[0], cos_x * kx_weight[None, :], precision=HIGHEST)
        - jnp.einsum("ykz,xk->zyx", moved[1], sin_x * kx_weight[None, :], precision=HIGHEST)
    ) * scale
    rim_rows = passed_along(potential[:, :margin, :], "gy", -1)
    potential = jnp.concatenate([potential, rim_rows], axis=1)
    rim_planes = passed_along(potential[:margin], "gz", -1)
    potential = jnp.concatenate([potential, rim_planes], axis=0)
    return interpolate(potential, qm_base, qm_frac, qm_charge, z_first, y_first)


def solution(mesh):
    in_specs = (
        P(None, ("gz", "gy")),
        P(None, ("gz", "gy")),
        P(None, ("gz", "gy")),
        P(None, ("gz", "gy")),
        P(("gz", "gy")),
    )
    out_specs = P(None, ("gz", "gy"))
    return jax.shard_map(shards, mesh=mesh, in_specs=in_specs, out_specs=out_specs, check_vma=False)
```

profile of v0, /device:TPU:0, one launch (start us, length us, event | category | flops | bytes accessed | tf_op | source)
XLA Modules:
  0.0 1281.5 jit_solution(2450267871987228641)
XLA Ops:
  7.1 158.1 %multiply_reduce_fusion = f32[27,195,4,1024]{3,2,1,0:T(4,128)} fusion(f32[4,195,1024]{2,1,0:T(8,128)S(1)} %fusion.18, f32[4,27,4,1024]{3,2,1,0:T(4,128)S(1)} %multiply_reduce_fusion.1), kind=kLoop, calls=%fused_computation | loop fusion | flops 150958080 | bytes 91226112 | tf_op jit(solution)/shard_map/reduce_sum | solution.py:101
  165.2 75.9 %dot_general.72 = f32[27,195,4096]{2,1,0:T(8,128)} reshape(f32[27,195,4,1024]{3,2,1,0:T(4,128)} %multiply_reduce_fusion) | data formatting | bytes 172523520 | tf_op jit(solution)/shard_map/dot_general | solution.py:102
  242.2 73.9 %fusion.6 = f32[27,195,384]{2,1,0:T(8,128)S(1)} fusion(f32[27,195,4096]{2,1,0:T(8,128)} %dot_general.72, pred[4096,384,1]{1,0,2:T(32,128)(4,1)S(1)} %fusion.280), kind=kOutput, calls=%fused_computation.18 | convolution fusion | flops 99373547520 | bytes 95921664 | tf_op jit(solution)/shard_map/dot_general | solution.py:102
  332.1 11.5 collective-permute-done.1
  344.8 9.8 convolution_bitcast_fusion
  374.1 11.4 copy.108
  385.5 80.2 %all_to_all.60 = f32[2,192,4608]{2,0,1:T(2,128)S(1)} all-to-all(f32[2,192,4608]{2,0,1:T(2,128)} %copy.108), channel_id=1, replica_groups=mesh['gz'=16,'gy'=2] {'gy'}, dimensions={1} | all-to-all | bytes 14155776 | tf_op jit(solution)/shard_map/all_to_all | solution.py:165
  476.6 10.3 fusion.44
  498.3 13.8 %fusion.42 = f32[384,96,24]{0,1,2:T(8,128)} fusion(f32[96,384,24]{1,0,2:T(8,128)} %copy.113), kind=kOutput, calls=%fused_computation.74 | convolution fusion | flops 4078190592 | bytes 7077888 | tf_op jit(solution)/shard_map/xyz,yk->kzx/dot_general | solution.py:77
  512.1 10.8 multiply_subtract_fusion
  531.8 14.2 %multiply_add_fusion = f32[384,96,24]{0,1,2:T(8,128)} fusion(f32[384,96,24]{0,1,2:T(8,128)} %fusion.42, f32[96,384,24]{1,0,2:T(8,128)S(1)} %copy.111), kind=kOutput, calls=%fused_computation.34 | convolution fusion | flops 4079960064 | bytes 10616832 | tf_op jit(solution)/shard_map/xyz,yk->kzx/dot_general | solution.py:78
  555.1 11.2 pad_maximum_fusion.1
  574.6 124.7 %all-to-all-done.1 = f32[2,384,2304]{2,0,1:T(2,128)} async-done(((f32[2,384,2304]{2,0,1:T(2,128)}), f32[2,384,2304]{2,0,1:T(2,128)}, u32[]{:S(2)}, u32[]{:S(2)}) %all-to-all-start.1) | async-done | bytes 7077920 | tf_op jit(solution)/shard_map/all_to_all | solution.py:172
  712.5 15.8 %fusion.40 = f32[24,96,384]{2,1,0:T(8,128)} fusion(f32[24,384,96]{2,1,0:T(8,128)} %squeeze.37), kind=kOutput, calls=%fused_computation.72 | convolution fusion | flops 4078190592 | bytes 7077888 | tf_op jit(solution)/shard_map/yzx,zk->yxk/dot_general | solution.py:75
  737.6 15.0 %fusion.38 = f32[24,96,384]{2,1,0:T(8,128)S(1)} fusion(f32[24,384,96]{2,1,0:T(8,128)} %squeeze.38), kind=kOutput, calls=%fused_computation.70 | convolution fusion | flops 4078190592 | bytes 7077888 | tf_op jit(solution)/shard_map/yzx,zk->yxk/dot_general | solution.py:77
  752.6 14.8 %subtract_multiply_fusion = f32[24,96,384]{2,1,0:T(8,128)S(1)} fusion(f32[24,96,384]{2,1,0:T(8,128)S(1)} %copy-done.9, f32[24,384,96]{2,1,0:T(8,128)} %squeeze.38, f32[96]{0:T(128)S(1)} %copy-done.41, f32[24,384]{1,0:T(8,128)S(1)} %copy-done.11, pred[96]{0:T(512)(128)(4,1)S(1)} %copy-done.42, pred[24,384]{1,0:T(8,128)(4,1)S(1)} %broadcast_or_fusion, ...), kind=kOutput, calls=%fused_computation.33 | convolution fusion | flops 4091461632 | bytes 10700640 | tf_op jit(solution)/shard_map/yzx,zk->yxk/dot_general | solution.py:76
  767.5 12.5 add_multiply_fusion.1
  789.2 10.7 fusion.46
  799.9 10.7 convolution_subtract_fusion
  819.5 13.8 %convolution_add_fusion = f32[384,24,96]{0,2,1:T(8,128)} fusion(f32[384,24,96]{0,2,1:T(8,128)} %fusion.46, f32[24,96,384]{2,1,0:T(8,128)S(1)} %subtract_multiply_fusion, s32[384]{0:T(512)S(1)} %add_select_fusion.7), kind=kOutput, calls=%fused_computation.47 | convolution fusion | flops 4079075328 | bytes 10618368 | tf_op jit(solution)/shard_map/yxk,kp->pyx/dot_general | solution.py:78
  842.6 11.2 pad_maximum_fusion.2
  853.9 31.3 %all-to-all-start.2 = ((f32[2,384,2304]{2,0,1:T(2,128)}), f32[2,384,2304]{2,0,1:T(2,128)}, u32[]{:S(2)}, u32[]{:S(2)}) async-start(f32[2,384,2304]{2,0,1:T(2,128)} %pad_maximum_fusion.2), calls=%async_computation.2 | async-start | bytes 14155776 | tf_op jit(solution)/shard_map/all_to_all | solution.py:194
  885.3 127.6 %all-to-all-done.2 = f32[2,384,2304]{2,0,1:T(2,128)} async-done(((f32[2,384,2304]{2,0,1:T(2,128)}), f32[2,384,2304]{2,0,1:T(2,128)}, u32[]{:S(2)}, u32[]{:S(2)}) %all-to-all-start.2) | async-done | bytes 7077920 | tf_op jit(solution)/shard_map/all_to_all | solution.py:194
  1028.6 10.3 fusion.80
  1038.8 10.4 fusion.74
  1086.2 12.3 copy.136
  1107.2 77.8 %all-to-all-done.3 = f32[2,384,2304]{2,0,1:T(2,128)} async-done(((f32[2,384,2304]{2,0,1:T(2,128)}), f32[2,384,2304]{2,0,1:T(2,128)}, u32[]{:S(2)}, u32[]{:S(2)}) %all-to-all-start.3) | async-done | bytes 7077920 | tf_op jit(solution)/shard_map/all_to_all | solution.py:207
  1200.0 12.9 %fusion.8 = f32[384,192,24]{0,1,2:T(8,128)S(1)} fusion(f32[192,192,24]{0,2,1:T(8,128)} %bitcast.186, f32[192]{0:T(256)S(1)} %compare_select_fusion.3), kind=kOutput, calls=%fused_computation.19 | convolution fusion | flops 4077600768 | bytes 10617600 | tf_op jit(solution)/shard_map/ykz,xk->zyx/dot_general | solution.py:213
  1213.0 10.8 multiply_bitcast_fusion
  1229.9 27.0 %collective-permute-start.3 = (f32[3,195,384]{2,1,0:T(8,128)S(1)}, f32[3,195,384]{2,1,0:T(8,128)S(1)}, u32[]{:S(2)}, u32[]{:S(2)}) collective-permute-start(f32[3,195,384]{2,1,0:T(8,128)S(1)} %pad_maximum_fusion.4), channel_id=1, source_target_pairs={{2,0},{4,2},{6,4},{8,6},{10,8},{12,10},{14,12},{16,14},{18,16},{20... | collective-permute-start | bytes 2695688 | tf_op jit(solution)/shard_map/ppermute | solution.py:19
  1258.1 9.8 collective-permute-done.3
  1267.9 11.8 fusion
  (193 shorter events, 227.9 us)
Async XLA Ops:
  165.2 75.9 %copy-start.12 = (s32[1,1024]{1,0:T(1,128)S(1)}, s32[1,1024]{1,0:T(1,128)}, u32[]{:S(2)}) copy-start(s32[1,1024]{1,0:T(1,128)} %get-tuple-element.46) | copy-start | bytes 12292
  316.1 7.3 collective-permute-start
  328.3 15.2 %collective-permute-start.1 = (f32[3,192,384]{2,1,0:T(8,128)S(1)}, f32[3,192,384]{2,1,0:T(8,128)S(1)}, u32[]{:S(2)}, u32[]{:S(2)}) collective-permute-start(f32[3,192,384]{2,1,0:T(8,128)S(1)} %slice.168), channel_id=1, source_target_pairs={{30,0},{0,2},{2,4},{4,6},{6,8},{8,10},{10,12},{12,14},{14,16},{16,... | collective-permute-start | bytes 2654216 | tf_op jit(solution)/shard_map/ppermute | solution.py:19
  566.4 133.0 %all-to-all-start.1 = ((f32[2,384,2304]{2,0,1:T(2,128)}), f32[2,384,2304]{2,0,1:T(2,128)}, u32[]{:S(2)}, u32[]{:S(2)}) async-start(f32[2,384,2304]{2,0,1:T(2,128)} %pad_maximum_fusion.1), calls=%async_computation.1 | async-start | bytes 14155776 | tf_op jit(solution)/shard_map/all_to_all | solution.py:172
  737.5 15.1 %copy-start.9 = (f32[24,96,384]{2,1,0:T(8,128)S(1)}, f32[24,96,384]{2,1,0:T(8,128)}, u32[]{:S(2)}) copy-start(f32[24,96,384]{2,1,0:T(8,128)} %fusion.40) | copy-start | bytes 10616836
  737.5 15.1 %copy-start.10 = (f32[24,384]{1,0:T(8,128)S(1)}, f32[24,384]{1,0:T(8,128)}, u32[]{:S(2)}) copy-start(f32[24,384]{1,0:T(8,128)} %broadcast_add_fusion) | copy-start | bytes 110596
  737.5 15.1 %copy-start.11 = (f32[24,384]{1,0:T(8,128)S(1)}, f32[24,384]{1,0:T(8,128)}, u32[]{:S(2)}) copy-start(f32[24,384]{1,0:T(8,128)} %broadcast_multiply_fusion) | copy-start | bytes 110596
  737.5 15.1 %copy-start.40 = (f32[96]{0:T(128)S(1)}, f32[96]{0:T(128)}, u32[]{:S(2)}) copy-start(f32[96]{0:T(128)} %get-tuple-element.81) | copy-start | bytes 1156
  737.5 15.1 %copy-start.41 = (f32[96]{0:T(128)S(1)}, f32[96]{0:T(128)}, u32[]{:S(2)}) copy-start(f32[96]{0:T(128)} %get-tuple-element.82) | copy-start | bytes 1156
  737.5 15.1 %copy-start.42 = (pred[96]{0:T(512)(128)(4,1)S(1)}, pred[96]{0:T(512)(128)(4,1)}, u32[]{:S(2)}) copy-start(pred[96]{0:T(512)(128)(4,1)} %fusion.189) | copy-start | bytes 292
  737.5 29.9 %slice-start = ((s8[4718592]{0:T(1024)(128)(4,1)}), s8[4194304]{0:T(1024)(128)(4,1)S(1)}, s32[]{:S(2)}) async-start(s8[4718592]{0:T(1024)(128)(4,1)} %bitcast.187), calls=%async_computation.4 | async-start | bytes 8388608
  752.6 14.8 %slice-start.1 = ((s8[4718592]{0:T(1024)(128)(4,1)}), s8[524288]{0:T(1024)(128)(4,1)S(1)}, s32[]{:S(2)}) async-start(s8[4718592]{0:T(1024)(128)(4,1)} %bitcast.187), calls=%async_computation.5 | async-start | bytes 1048576
  853.9 159.0 %all-to-all-start.2 = ((f32[2,384,2304]{2,0,1:T(2,128)}), f32[2,384,2304]{2,0,1:T(2,128)}, u32[]{:S(2)}, u32[]{:S(2)}) async-start(f32[2,384,2304]{2,0,1:T(2,128)} %pad_maximum_fusion.2), calls=%async_computation.2 | async-start | bytes 14155776 | tf_op jit(solution)/shard_map/all_to_all | solution.py:194
  1098.6 86.5 %all-to-all-start.3 = ((f32[2,384,2304]{2,0,1:T(2,128)}), f32[2,384,2304]{2,0,1:T(2,128)}, u32[]{:S(2)}, u32[]{:S(2)}) async-start(f32[2,384,2304]{2,0,1:T(2,128)} %copy.136), calls=%async_computation.3 | async-start | bytes 14155776 | tf_op jit(solution)/shard_map/all_to_all | solution.py:207
  1223.9 5.9 collective-permute-start.2
  1224.1 33.2 %copy-start.16 = (f32[1,128]{1,0:T(1,128)S(1)}, f32[1,128]{1,0:T(1,128)}, u32[]{:S(2)}) copy-start(f32[1,128]{1,0:T(1,128)} %get-tuple-element.71) | copy-start | bytes 1540
  1224.1 33.2 %copy-start.22 = (f32[1,128]{1,0:T(1,128)S(1)}, f32[1,128]{1,0:T(1,128)}, u32[]{:S(2)}) copy-start(f32[1,128]{1,0:T(1,128)} %get-tuple-element.57) | copy-start | bytes 1540
  1224.1 33.2 %copy-start.23 = (f32[1,128]{1,0:T(1,128)S(1)}, f32[1,128]{1,0:T(1,128)}, u32[]{:S(2)}) copy-start(f32[1,128]{1,0:T(1,128)} %get-tuple-element.58) | copy-start | bytes 1540
  1224.1 33.2 %copy-start.24 = (f32[1,128]{1,0:T(1,128)S(1)}, f32[1,128]{1,0:T(1,128)}, u32[]{:S(2)}) copy-start(f32[1,128]{1,0:T(1,128)} %get-tuple-element.59) | copy-start | bytes 1540
  1224.1 33.2 %copy-start.25 = (f32[1,128]{1,0:T(1,128)S(1)}, f32[1,128]{1,0:T(1,128)}, u32[]{:S(2)}) copy-start(f32[1,128]{1,0:T(1,128)} %get-tuple-element.63) | copy-start | bytes 1540
  1224.1 33.2 %copy-start.26 = (f32[1,128]{1,0:T(1,128)S(1)}, f32[1,128]{1,0:T(1,128)}, u32[]{:S(2)}) copy-start(f32[1,128]{1,0:T(1,128)} %get-tuple-element.64) | copy-start | bytes 1540
  1224.1 33.2 %copy-start.27 = (f32[1,128]{1,0:T(1,128)S(1)}, f32[1,128]{1,0:T(1,128)}, u32[]{:S(2)}) copy-start(f32[1,128]{1,0:T(1,128)} %get-tuple-element.65) | copy-start | bytes 1540
  1224.1 33.2 %copy-start.28 = (f32[1,128]{1,0:T(1,128)S(1)}, f32[1,128]{1,0:T(1,128)}, u32[]{:S(2)}) copy-start(f32[1,128]{1,0:T(1,128)} %get-tuple-element.66) | copy-start | bytes 1540
  1224.1 33.2 %copy-start.14 = (f32[1,128]{1,0:T(1,128)S(1)}, f32[1,128]{1,0:T(1,128)}, u32[]{:S(2)}) copy-start(f32[1,128]{1,0:T(1,128)} %get-tuple-element.73) | copy-start | bytes 1540
  1224.1 33.2 %copy-start.15 = (f32[1,128]{1,0:T(1,128)S(1)}, f32[1,128]{1,0:T(1,128)}, u32[]{:S(2)}) copy-start(f32[1,128]{1,0:T(1,128)} %get-tuple-element.75) | copy-start | bytes 1540
  1224.2 33.2 %copy-start.17 = (f32[1,128]{1,0:T(1,128)S(1)}, f32[1,128]{1,0:T(1,128)}, u32[]{:S(2)}) copy-start(f32[1,128]{1,0:T(1,128)} %get-tuple-element.49) | copy-start | bytes 1540
  1224.2 33.2 %copy-start.18 = (f32[1,128]{1,0:T(1,128)S(1)}, f32[1,128]{1,0:T(1,128)}, u32[]{:S(2)}) copy-start(f32[1,128]{1,0:T(1,128)} %get-tuple-element.60) | copy-start | bytes 1540
  1224.2 33.2 %copy-start.19 = (f32[1,128]{1,0:T(1,128)S(1)}, f32[1,128]{1,0:T(1,128)}, u32[]{:S(2)}) copy-start(f32[1,128]{1,0:T(1,128)} %get-tuple-element.61) | copy-start | bytes 1540
  1224.2 33.2 %copy-start.20 = (f32[1,128]{1,0:T(1,128)S(1)}, f32[1,128]{1,0:T(1,128)}, u32[]{:S(2)}) copy-start(f32[1,128]{1,0:T(1,128)} %get-tuple-element.62) | copy-start | bytes 1540
  1224.2 33.2 %copy-start.21 = (f32[1,128]{1,0:T(1,128)S(1)}, f32[1,128]{1,0:T(1,128)}, u32[]{:S(2)}) copy-start(f32[1,128]{1,0:T(1,128)} %get-tuple-element.67) | copy-start | bytes 1540
  1224.2 33.3 %copy-start.37 = (s32[128]{0:T(128)S(1)}, s32[128]{0:T(128)}, u32[]{:S(2)}) copy-start(s32[128]{0:T(128)} %get-tuple-element.68) | copy-start | bytes 1540
  1229.9 38.0 %collective-permute-start.3 = (f32[3,195,384]{2,1,0:T(8,128)S(1)}, f32[3,195,384]{2,1,0:T(8,128)S(1)}, u32[]{:S(2)}, u32[]{:S(2)}) collective-permute-start(f32[3,195,384]{2,1,0:T(8,128)S(1)} %pad_maximum_fusion.4), channel_id=1, source_target_pairs={{2,0},{4,2},{6,4},{8,6},{10,8},{12,10},{14,12},{16,14},{18,16},{20... | collective-permute-start | bytes 2695688 | tf_op jit(solution)/shard_map/ppermute | solution.py:19
  (20 other events, 190.4 us)
where the time goes:
time: 1290 us; the launch traced here: 1280 us
  waiting for transfers between devices  357 us (28%)
  matrix products  320 us (25%)
  local copies, waits for them, and re-layouts  245 us (19%)
  other arithmetic  205 us (16%)
  blocking collectives  80.2 us (6%)
  starting transfers between devices  73.5 us (6%)
    all_to_all x2, waiting for transfers between devices, shards(): lax.all_to_all(packed, 'gz', split_axis=1, concat_axis=2, tiled=True)  252 us
    reduce_sum x1, other arithmetic, spread_grid(): jnp.sum(by_plane[:, :, None, :, :] * row_hits[:, None, :, None, :], axis=0)  158 us
    all_to_all x1, blocking collectives, shards(): lax.all_to_all(packed, 'gy', split_axis=1, concat_axis=2, tiled=True)  80.2 us
    all_to_all x1, waiting for transfers between devices, shards(): lax.all_to_all(packed, 'gy', split_axis=1, concat_axis=2, tiled=True)  77.8 us
    dot_general x1, local copies, waits for them, and re-layouts, spread_grid(): jnp.dot(placed.reshape(z_extent * y_extent, ORDER * count), column_hits.r...  75.9 us
    dot_general x1, matrix products, spread_grid(): jnp.dot(placed.reshape(z_extent * y_extent, ORDER * count), column_hits.r...  73.9 us
    dot_general x3, matrix products, transform(): fourth = jnp.einsum(form, real_part, sine, precision=HIGHEST)  40.4 us
    unnamed x4, matrix products  39.6 us
  transfers between devices with their start and end apart: 7, of which 7 were waited for; matrix products, arithmetic and copies ran while one was open for 1% of the time, Pallas kernels for 0%

commit v1 on v0

v1 whole, which is shorter than its diff:
```python
import math

import jax
import jax.numpy as jnp
import numpy as np
from jax import lax
from jax.experimental import pallas as pl
from jax.experimental.pallas import tpu as pltpu
from jax.sharding import PartitionSpec as P

GRID = 384
ORDER = 4
SPLITTING = 0.8
AXES = ("gz", "gy")
RADIX = 3


def round_up(value, unit):
    return -(-value // unit) * unit


def window_start(z_part, z_local):
    return pl.multiple_of(z_part * z_local // 8 * 8, 8)


def spline_weights(frac):
    remain = 1.0 - frac
    square = frac * frac
    cubed = square * frac
    values = [
        remain * remain * remain / 6.0,
        (3.0 * cubed - 6.0 * square + 4.0) / 6.0,
        (-3.0 * cubed + 3.0 * square + 3.0 * frac + 1.0) / 6.0,
        cubed / 6.0,
    ]
    slopes = [
        -0.5 * remain * remain,
        (3.0 * square - 4.0 * frac) / 2.0,
        (-3.0 * square + 2.0 * frac + 1.0) / 2.0,
        0.5 * square,
    ]
    return values, slopes


def sine_of_turns(turn):
    square = turn * turn
    total = jnp.full_like(turn, 0.0)
    for power in range(6, -1, -1):
        term = (-1.0) ** power * (2.0 * math.pi) ** (2 * power + 1) / math.factorial(2 * power + 1)
        total = total * square + term
    return total * turn


def cos_sin_of_turns(turn):
    folded = jnp.minimum(jnp.maximum(turn, -0.5 - turn), 0.5 - turn)
    return sine_of_turns(0.25 - jnp.abs(turn)), sine_of_turns(folded)


def halves(value):
    high = value.astype(jnp.bfloat16)
    low = (value - high.astype(jnp.float32)).astype(jnp.bfloat16)
    return high, low


def dot(left, right, contract=((1,), (0,))):
    return lax.dot_general(left, right, (contract, ((), ())), preferred_element_type=jnp.float32)


def x_phases(cells, kx_column, points):
    product = kx_column * cells
    turn = product * (1.0 / points)
    rest = product - points * jnp.floor(turn + 0.5)
    return cos_sin_of_turns(rest * (1.0 / points))


def spread_kernel(kx_ref, rec_ref, out_ref, *, points, z_local, y_local, count_y, kx_here, z_rows, y_rows):
    step = pl.program_id(0)
    z_part = step // count_y
    y_part = step % count_y
    atoms = rec_ref.shape[2]
    cells = ORDER**3

    @pl.when(step == 0)
    def _():
        out_ref[...] = jnp.zeros_like(out_ref)

    start = window_start(z_part, z_local)
    first_z = start.astype(jnp.float32)
    first_y = (y_part * y_local).astype(jnp.float32)
    local_z = (rec_ref[0, cells : cells + 1, :] - first_z).astype(jnp.int32)
    local_y = (rec_ref[0, cells + 1 : cells + 2, :] - first_y).astype(jnp.int32)
    x_cell = rec_ref[0, cells + 2 : cells + 3, :]
    kx_column = kx_ref[:, 0:1]
    base_cos, base_sin = x_phases(x_cell, kx_column, points)
    phase_re, phase_im = [base_cos], [-base_sin]
    for c in range(1, ORDER):
        turn_cos = kx_ref[:, 2 * c : 2 * c + 1]
        turn_sin = kx_ref[:, 2 * c + 1 : 2 * c + 2]
        phase_re.append(base_cos * turn_cos - base_sin * turn_sin)
        phase_im.append(-(base_sin * turn_cos + base_cos * turn_sin))
    z_iota = lax.broadcasted_iota(jnp.int32, (z_rows, atoms), 0)
    offset_z = z_iota - local_z
    y_iota = lax.broadcasted_iota(jnp.int32, (y_rows, atoms), 0)
    offset_y = y_iota - local_y
    masks = [offset_z == a for a in range(ORDER)]
    total = None
    for b in range(ORDER):
        pieces = [[], []]
        lines = []
        for a in range(ORDER):
            re = im = None
            for c in range(ORDER):
                row = a * ORDER * ORDER + b * ORDER + c
                weight = rec_ref[0, row : row + 1, :]
                re = weight * phase_re[c] if re is None else re + weight * phase_re[c]
                im = weight * phase_im[c] if im is None else im + weight * phase_im[c]
            lines.append((re, im))
        rows_hi, rows_lo = [], []
        for part in range(2):
            for k in range(kx_here):
                value = jnp.zeros((z_rows, atoms), jnp.float32)
                for a in range(ORDER):
                    value = jnp.where(masks[a], lines[a][part][k : k + 1, :], value)
                high, low = halves(value)
                rows_hi.append(high)
                rows_lo.append(low)
        hits = (offset_y == b).astype(jnp.float32).astype(jnp.bfloat16)
        stacked = jnp.concatenate(rows_hi + rows_lo, axis=0)
        product = dot(stacked, hits, ((1,), (1,)))
        total = product if total is None else total + product
    half = 2 * kx_here * z_rows
    for n in range(2 * kx_here):
        piece = total[n * z_rows : (n + 1) * z_rows] + total[half + n * z_rows : half + (n + 1) * z_rows]
        out_ref[y_part, n, pl.ds(start, z_rows), :] += piece


def split_dot(value, high, low):
    top, rest = halves(value)
    return dot(top, high) + (dot(rest, high) + dot(top, low))


def split_dot_left(high, low, value):
    top, rest = halves(value)
    return dot(high, top) + (dot(high, rest) + dot(low, top))


HALF_ROOT = math.sqrt(3.0) / 2.0


def three_way(parts, sign):
    (ar, ai), (br, bi), (cr, ci) = parts
    sum_r, sum_i = br + cr, bi + ci
    dif_r, dif_i = (br - cr) * HALF_ROOT, (bi - ci) * HALF_ROOT
    mid_r, mid_i = ar - 0.5 * sum_r, ai - 0.5 * sum_i
    return [
        (ar + sum_r, ai + sum_i),
        (mid_r - sign * dif_i, mid_i + sign * dif_r),
        (mid_r + sign * dif_i, mid_i - sign * dif_r),
    ]


def turned(value, cosine, sine, sign):
    re, im = value
    return (re * cosine - sign * (im * sine), im * cosine + sign * (re * sine))


def transform_kernel(
    scal_ref, re_ref, im_ref, right_hi, right_lo, left_hi, left_lo, tw_row, tw_col, row_ref, col_ref,
    out_ref, *, points, y_local, count_y, third,
):
    index = pl.program_id(0)
    z_pad = re_ref.shape[2]
    y_rows = re_ref.shape[3]

    def whole(ref):
        plane = None
        for q in range(count_y):
            piece = ref[q, 0]
            body = piece[:points]
            spare = z_pad - points
            body = jnp.concatenate([body[:spare] + piece[points:], body[spare:]], axis=0)
            if y_rows < points:
                body = jnp.concatenate(
                    [body, jnp.zeros((points, points - y_rows), jnp.float32)], axis=1
                )
            if q > 0:
                body = pltpu.roll(body, q * y_local, 1)
            plane = body if plane is None else plane + body
        return plane

    def lanes(value, part):
        return tuple(v[:, part * third : (part + 1) * third] for v in value)

    def rows(value, part):
        return tuple(v[part * third : (part + 1) * third] for v in value)

    plane = (whole(re_ref), whole(im_ref))
    parts = three_way([lanes(plane, n) for n in range(RADIX)], -1.0)
    done = []
    for n, part in enumerate(parts):
        if n > 0:
            part = turned(part, tw_row[2 * n : 2 * n + 1, :], tw_row[2 * n + 1 : 2 * n + 2, :], -1.0)
        done.append(split_dot(jnp.concatenate(part, axis=1), right_hi[...], right_lo[...]))
    parts = three_way(
        [
            (
                jnp.concatenate([d[n * third : (n + 1) * third, :third] for d in done], axis=1),
                jnp.concatenate([d[n * third : (n + 1) * third, third:] for d in done], axis=1),
            )
            for n in range(RADIX)
        ],
        -1.0,
    )
    scale = scal_ref[index, 0]
    square = scal_ref[index, 1]
    back = []
    for n, part in enumerate(parts):
        if n > 0:
            cosine = jnp.concatenate([tw_col[2 * n]] * RADIX, axis=1)
            sine = jnp.concatenate([tw_col[2 * n + 1]] * RADIX, axis=1)
            part = turned(part, cosine, sine, -1.0)
        spectrum = split_dot_left(left_hi[...], left_lo[...], jnp.concatenate(part, axis=0))
        col_factor = jnp.concatenate([col_ref[0, n * third : (n + 1) * third, :]] * RADIX, axis=1)
        col_square = jnp.concatenate([col_ref[1, n * third : (n + 1) * third, :]] * RADIX, axis=1)
        total = col_square + row_ref[1:2, :] + square
        safe = jnp.where(total > 0.0, total, 1.0)
        green = jnp.where(total > 0.0, col_factor * row_ref[0:1, :] * scale / (math.pi * safe), 0.0)
        swapped = jnp.concatenate([spectrum[third:] * green, spectrum[:third] * green], axis=0)
        result = split_dot_left(left_hi[...], left_lo[...], swapped)
        part = (result[third:], result[:third])
        if n > 0:
            part = turned(part, cosine, sine, 1.0)
        back.append(part)
    back = three_way(back, 1.0)
    plane = tuple(jnp.concatenate([b[i] for b in back], axis=0) for i in range(2))
    parts = []
    for n in range(RADIX):
        re, im = lanes(plane, n)
        result = split_dot(jnp.concatenate([im, re], axis=1), right_hi[...], right_lo[...])
        part = (result[:, third:], result[:, :third])
        if n > 0:
            part = turned(part, tw_row[2 * n : 2 * n + 1, :], tw_row[2 * n + 1 : 2 * n + 2, :], 1.0)
        parts.append(part)
    parts = three_way(parts, 1.0)
    spare = out_ref.shape[2] - points
    for i in range(2):
        value = jnp.concatenate([p[i] for p in parts], axis=1)
        out_ref[i, 0, :points, :] = value
        out_ref[i, 0, points:, :] = value[:spare]


def force_kernel(kx_ref, qm_ref, pot_ref, out_ref, *, points, z_local, count_y, kx_here, z_rows):
    step = pl.program_id(0)
    z_part = step // count_y
    atoms = qm_ref.shape[2]
    start = window_start(z_part, z_local)
    first_z = start.astype(jnp.float32)
    local_z = (qm_ref[0, 0:1, :] - first_z).astype(jnp.int32)
    cell_y = qm_ref[0, 1:2, :].astype(jnp.int32)
    x_cell = qm_ref[0, 2:3, :]
    w_z, d_z = spline_weights(qm_ref[0, 3:4, :])
    w_y, d_y = spline_weights(qm_ref[0, 4:5, :])
    w_x, d_x = spline_weights(qm_ref[0, 5:6, :])

    def placed(offset, weights):
        value = jnp.zeros(offset.shape, jnp.float32)
        for a in range(ORDER):
            value = jnp.where(offset == a, weights[a], value)
        return value

    offset_z = lax.broadcasted_iota(jnp.int32, (z_rows, atoms), 0) - local_z
    plane_w, plane_d = placed(offset_z, w_z), placed(offset_z, d_z)
    offset_y = lax.broadcasted_iota(jnp.int32, (points, atoms), 0) - cell_y
    offset_y = jnp.where(offset_y < 0, offset_y + points, offset_y)
    row_hi, row_lo = halves(jnp.concatenate([placed(offset_y, w_y), placed(offset_y, d_y)], axis=1))
    base_cos, base_sin = x_phases(x_cell, kx_ref[:, 0:1], points)
    line_w = [w_x[0] * base_cos, w_x[0] * base_sin]
    line_d = [d_x[0] * base_cos, d_x[0] * base_sin]
    for c in range(1, ORDER):
        turn_cos = kx_ref[:, 2 * c : 2 * c + 1]
        turn_sin = kx_ref[:, 2 * c + 1 : 2 * c + 2]
        cosine = base_cos * turn_cos - base_sin * turn_sin
        sine = base_sin * turn_cos + base_cos * turn_sin
        line_w = [line_w[0] + w_x[c] * cosine, line_w[1] + w_x[c] * sine]
        line_d = [line_d[0] + d_x[c] * cosine, line_d[1] + d_x[c] * sine]
    force = [jnp.zeros((1, atoms), jnp.float32) for _ in range(3)]
    window = jnp.concatenate(
        [pot_ref[i, k, pl.ds(start, z_rows), :] for k in range(kx_here) for i in range(2)], axis=0
    )
    top, rest = halves(window)
    along = dot(top, row_hi) + (dot(rest, row_hi) + dot(top, row_lo))
    for k in range(kx_here):
        for i in range(2):
            n = (2 * k + i) * z_rows
            plain, sloped = along[n : n + z_rows, :atoms], along[n : n + z_rows, atoms:]
            sign = 1.0 if i == 0 else -1.0
            sum_z = jnp.sum(plain * plane_d, axis=0, keepdims=True)
            sum_y = jnp.sum(sloped * plane_w, axis=0, keepdims=True)
            sum_x = jnp.sum(plain * plane_w, axis=0, keepdims=True)
            across = line_w[i][k : k + 1, :] * sign
            force[0] += sum_z * across
            force[1] += sum_y * across
            force[2] += sum_x * (line_d[i][k : k + 1, :] * sign)
    out_ref[0] = jnp.concatenate(force, axis=0)


def tables(points):
    third = points // RADIX
    index = np.arange(third)
    angle = 2.0 * np.pi / third * (np.outer(index, index) % third)
    cosine, sine = np.cos(angle), np.sin(angle)
    right = np.block([[cosine, -sine], [sine, cosine]])
    left = np.block([[cosine, sine], [-sine, cosine]])

    def split(matrix):
        value = jnp.asarray(matrix, jnp.float32)
        high = jnp.asarray(matrix.astype(jnp.bfloat16))
        low = jnp.asarray((matrix - matrix.astype(jnp.bfloat16).astype(np.float64)).astype(jnp.bfloat16))
        return high, low

    turn = 2.0 * np.pi / points * np.outer(np.arange(RADIX), index)
    twiddle = np.stack([np.cos(turn), np.sin(turn)], axis=1).reshape(2 * RADIX, third).astype(np.float32)
    tw_row = jnp.asarray(twiddle)
    tw_col = jnp.asarray(np.broadcast_to(twiddle[:, :, None], (2 * RADIX, third, third)).copy())
    slots = (RADIX * np.arange(third)[None, :] + np.arange(RADIX)[:, None]).reshape(-1)
    factor, square = factors(slots, points)
    row = jnp.asarray(np.stack([factor, square]).astype(np.float32))
    col = jnp.asarray(
        np.broadcast_to(np.stack([factor, square])[:, :, None], (2, points, third)).astype(np.float32)
    )
    return split(right) + split(left) + (tw_row, tw_col, row, col)


def factors(index, points):
    signed = np.where(index < points // 2, index, index - points) / points
    spline = 2.0 / 3.0 + np.cos(2.0 * np.pi * index / points) / 3.0
    factor = np.exp(-((np.pi / SPLITTING) ** 2) * signed**2) / spline**2
    return np.where(index == points // 2, 0.0, factor), signed**2


def shards(spread_weights, spread_base, qm_base, qm_frac, qm_charge):
    points = GRID
    count_z = lax.axis_size("gz")
    count_y = lax.axis_size("gy")
    devices = count_z * count_y
    z_local = points // count_z
    y_local = points // count_y
    kx_here = -(-(points // 2) // devices)
    here = lax.axis_index("gz") * count_y + lax.axis_index("gy")
    kx = here * kx_here + jnp.arange(kx_here, dtype=jnp.int32)
    z_rows = round_up(z_local + ORDER - 1 + (0 if z_local % 8 == 0 else 7), 8)
    z_pad = (points - z_local) // 8 * 8 + z_rows
    y_rows = min(round_up(y_local + ORDER - 1, 128), points)

    atoms = spread_weights.shape[1]
    qms = qm_charge.shape[0]
    qm_rows = jnp.concatenate([qm_base.astype(jnp.float32), qm_frac], axis=0).reshape(-1)
    lines = -(-qm_rows.shape[0] // atoms)
    qm_rows = jnp.pad(qm_rows, (0, lines * atoms - qm_rows.shape[0])).reshape(lines, atoms)
    record = jnp.concatenate([spread_weights, spread_base.astype(jnp.float32), qm_rows], axis=0)
    held = round_up(record.shape[0], 8)
    record = jnp.pad(record, ((0, held - record.shape[0]), (0, 0)))
    records = lax.all_gather(record, AXES, axis=0, tiled=False)

    fkx = kx.astype(jnp.float32)
    turn = 2.0 * math.pi / points * ((kx[:, None] * jnp.arange(ORDER)[None, :]) % points).astype(jnp.float32)
    kx_table = jnp.stack([jnp.cos(turn), jnp.sin(turn)], axis=2).reshape(kx_here, 2 * ORDER)
    kx_table = kx_table.at[:, 0].set(fkx)

    spread = pl.pallas_call(
        lambda *refs: spread_kernel(
            *refs, points=points, z_local=z_local, y_local=y_local, count_y=count_y,
            kx_here=kx_here, z_rows=z_rows, y_rows=y_rows,
        ),
        grid=(devices,),
        in_specs=[
            pl.BlockSpec(kx_table.shape, lambda d: (0, 0)),
            pl.BlockSpec((1, held, atoms), lambda d: (d, 0, 0)),
        ],
        out_specs=pl.BlockSpec((count_y, 2 * kx_here, z_pad, y_rows), lambda d: (0, 0, 0, 0)),
        out_shape=jax.ShapeDtypeStruct((count_y, 2 * kx_here, z_pad, y_rows), jnp.float32),
        compiler_params=pltpu.CompilerParams(
            dimension_semantics=("arbitrary",), vmem_limit_bytes=60 * 1024 * 1024
        ),
        name="spread",
    )(kx_table, records)

    signed = fkx / points
    spline = 2.0 / 3.0 + jnp.cos(2.0 * math.pi / points * fkx) / 3.0
    kx_factor = jnp.exp(-((math.pi / SPLITTING) ** 2) * signed * signed) / (spline * spline)
    kx_factor = kx_factor * jnp.where(kx == 0, 1.0, 2.0) / float(points) ** 3
    kx_factor = jnp.where(kx < points // 2, kx_factor, 0.0)
    scalars = jnp.stack([kx_factor, signed * signed], axis=1)
    constants = tables(points)
    third = points // RADIX

    def fixed(array):
        return pl.BlockSpec(array.shape, lambda k, n=array.ndim: (0,) * n)

    block = (count_y, 1, z_pad, y_rows)
    potential = pl.pallas_call(
        lambda *refs: transform_kernel(
            *refs, points=points, y_local=y_local, count_y=count_y, third=third
        ),
        grid=(kx_here,),
        in_specs=[
            pl.BlockSpec(memory_space=pltpu.SMEM),
            pl.BlockSpec(block, lambda k: (0, k, 0, 0)),
            pl.BlockSpec(block, lambda k: (0, k + kx_here, 0, 0)),
        ]
        + [fixed(array) for array in constants],
        out_specs=pl.BlockSpec((2, 1, z_pad, points), lambda k: (0, k, 0, 0)),
        out_shape=jax.ShapeDtypeStruct((2, kx_here, z_pad, points), jnp.float32),
        compiler_params=pltpu.CompilerParams(
            dimension_semantics=("arbitrary",), vmem_limit_bytes=60 * 1024 * 1024
        ),
        name="transform",
    )(scalars, spread, spread, *constants)

    first_line = ORDER**3 + 3
    qm_all = records[:, first_line : first_line + lines, :].reshape(devices, lines * atoms)
    qm_all = qm_all[:, : 6 * qms].reshape(devices, 6, qms)
    partial = pl.pallas_call(
        lambda *refs: force_kernel(
            *refs, points=points, z_local=z_local, count_y=count_y, kx_here=kx_here, z_rows=z_rows
        ),
        grid=(devices,),
        in_specs=[
            pl.BlockSpec(kx_table.shape, lambda d: (0, 0)),
            pl.BlockSpec((1, 6, qms), lambda d: (d, 0, 0)),
            pl.BlockSpec((2, kx_here, z_pad, points), lambda d: (0, 0, 0, 0)),
        ],
        out_specs=pl.BlockSpec((1, 3, qms), lambda d: (d, 0, 0)),
        out_shape=jax.ShapeDtypeStruct((devices, 3, qms), jnp.float32),
        compiler_params=pltpu.CompilerParams(
            dimension_semantics=("arbitrary",), vmem_limit_bytes=60 * 1024 * 1024
        ),
        name="forces",
    )(kx_table, qm_all, potential)
    moved = lax.all_to_all(partial, AXES, split_axis=0, concat_axis=0, tiled=True)
    return -qm_charge[None, :] * jnp.sum(moved, axis=0)


def solution(mesh):
    in_specs = (
        P(None, AXES),
        P(None, AXES),
        P(None, AXES),
        P(None, AXES),
        P(AXES),
    )
    out_specs = P(None, AXES)
    return jax.shard_map(shards, mesh=mesh, in_specs=in_specs, out_specs=out_specs, check_vma=False)
```

time: 1290 us -> 272 us (0.21)
  matrix products: 320 us -> 0 us
  waiting for transfers between devices: 357 us -> 89.7 us
  local copies, waits for them, and re-layouts: 245 us -> 2.2 us
  other arithmetic: 205 us -> 6.48 us
  Pallas kernels: 0 us -> 155 us
  blocking collectives: 80.2 us -> 0 us
  starting transfers between devices: 73.5 us -> 3.12 us
    all_to_all x3 -> x1, waiting for transfers between devices: 330 us -> 7.59 us  [shards(): lax.all_to_all(partial, AXES, split_axis=0, concat_axis=0, tiled=True)]
    dot_general x18 -> x0, matrix products: 280 us -> none  [the longest x1 73.9 us: spread_grid(): jnp.dot(placed.reshape(z_extent * y_extent, ORDER * count), column_hits.r...]
    reduce_sum x6 -> x1, other arithmetic: 163 us -> 0.04 us  [shards(): return -qm_charge[None, :] * jnp.sum(moved, axis=0)]
    pallas_call x0 -> x3, Pallas kernels: none -> 155 us  [the longest x1 104 us: shards(): pl.pallas_call(lambda *refs: spread_kernel(*refs, points=points, z_local=...]
    all_gather x0 -> x1, waiting for transfers between devices: none -> 82.1 us  [shards(): records = lax.all_gather(record, AXES, axis=0, tiled=False)]
    all_to_all x1 -> x0, blocking collectives: 80.2 us -> none  [shards(): lax.all_to_all(packed, 'gy', split_axis=1, concat_axis=2, tiled=True)]
    dot_general x2 -> x0, local copies, waits for them, and re-layouts: 76 us -> none  [the longest x1 75.9 us: spread_grid(): jnp.dot(placed.reshape(z_extent * y_extent, ORDER * count), column_hits.r...]
    another operation x6 -> x1, local copies, waits for them, and re-layouts: 60.1 us -> 0.01 us  [shards(): jnp.stack([jnp.cos(turn), jnp.sin(turn)], axis=2)]
  transfers between devices with their start and end apart: 7 -> 2, of which waited for: 7 -> 2; matrix products, arithmetic and copies ran while one was open for 1% -> 1% of each run, Pallas kernels for 0% -> 0%
where the time goes in v1:
time: 272 us; the launch traced here: 270 us
  Pallas kernels  155 us (57%)
  waiting for transfers between devices  89.7 us (33%)
  between operations  13.5 us (5%)
  other arithmetic  6.48 us (2%)
  starting transfers between devices  3.12 us (1%)
    pallas_call x1, Pallas kernels, shards(): pl.pallas_call(lambda *refs: spread_kernel(*refs, points=points, z_local=...  104 us
    all_gather x1, waiting for transfers between devices, shards(): records = lax.all_gather(record, AXES, axis=0, tiled=False)  82.1 us
    pallas_call x1, Pallas kernels, shards(): pl.pallas_call(lambda *refs: transform_kernel(*refs, points=points, y_loc...  26.6 us
    pallas_call x1, Pallas kernels, shards(): pl.pallas_call(lambda *refs: force_kernel(*refs, points=points, z_local=z...  24.5 us
    all_to_all x1, waiting for transfers between devices, shards(): lax.all_to_all(partial, AXES, split_axis=0, concat_axis=0, tiled=True)  7.59 us
  transfers between devices with their start and end apart: 2, of which 2 were waited for; matrix products, arithmetic and copies ran while one was open for 1% of the time, Pallas kernels for 0%

profile of v1, /device:TPU:0, one launch (start us, length us, event | category | flops | bytes accessed | tf_op | source)
XLA Modules:
  0.0 270.5 jit_solution(16915707642963458694)
XLA Ops:
  6.5 0.0 all-gather.3.cloned.1.call-start
  6.5 0.7 convert_element_type.44
  7.2 0.7 convert_element_type.43
  7.9 0.7 maximum_bitcast_fusion
  8.6 1.7 select_maximum_fusion
  10.3 0.0 all-gather.3.cloned.1.call-update
  10.4 0.1 fusion.9
  10.4 0.1 copy.27
  10.5 0.6 compare_reduce_fusion
  11.2 0.7 multiply_select_fusion
  11.9 0.1 scatter.4.refs_0_
  11.9 0.0 copy-start
  12.0 0.7 pad_maximum_fusion.1.refs_0_
  12.6 82.1 %all-gather.3.cloned.1.call-done = f32[2304,1024]{1,0:T(8,128)} async-done(((f32[72,1024]{1,0:T(8,128)}), f32[2304,1024]{1,0:T(8,128)}) %all-gather.3.cloned.1.call-update) | async-done | bytes 9437200 | tf_op jit(solution)/shard_map/all_gather | solution.py:363
  94.7 1.3 slice.26
  96.1 0.7 reshape.195.refs_1_
  96.8 0.0 copy-done
  96.8 104.4 %spread.1.refs_1_.refs_2_ = f32[2,12,392,256]{3,2,1,0:T(8,128)} custom-call(f32[6,8]{1,0:T(8,128)} %copy-done, f32[32,72,1024]{2,1,0:T(8,128)} %bitcast.9), custom_call_target="tpu_custom_call" | custom-call | tf_op jit(solution)/shard_map/spread/pallas_call | solution.py:370
  201.2 0.0 copy-start.1
  201.2 26.6 %transform.1.refs_2_ = f32[2,6,392,384]{3,2,1,0:T(8,128)} custom-call(f32[6,2]{1,0:T(8,128)} %pad_maximum_fusion.1.refs_0_, f32[2,12,392,256]{3,2,1,0:T(8,128)} %spread.1.refs_1_.refs_2_, f32[2,12,392,256]{3,2,1,0:T(8,128)} %spread.1.refs_1_.refs_2_, bf16[256,256]{1,0:T(8,128)(2,1)} %constant.101.clone.refs_3_, bf16[256,256]{1,0:T(8,128)(2,1)} %constant.102.clone.refs_4_, ...), custom_call_target="tpu_custom_call" | custom-call | tf_op jit(solution)/shard_map/transform/pallas_call | solution.py:401
  227.8 24.5 %forces.1 = f32[32,3,128]{2,1,0:T(4,128)} custom-call(f32[6,8]{1,0:T(8,128)} %copy-done, f32[32,6,128]{2,1,0:T(8,128)} %reshape.195.refs_1_, f32[2,6,392,384]{3,2,1,0:T(8,128)} %transform.1.refs_2_), custom_call_target="tpu_custom_call" | custom-call | tf_op jit(solution)/shard_map/forces/pallas_call | solution.py:423
  252.3 3.1 %all-to-all-start = ((f32[32,3,128]{2,1,0:T(4,128)}), f32[32,3,128]{2,1,0:T(4,128)S(1)}, u32[]{:S(2)}, u32[]{:S(2)}) async-start(f32[32,3,128]{2,1,0:T(4,128)} %forces.1), calls=%async_computation | async-start | bytes 131072 | tf_op jit(solution)/shard_map/all_to_all | solution.py:440
  255.4 0.0 copy-done.1
  255.4 7.6 %all-to-all-done = f32[32,3,128]{2,1,0:T(4,128)S(1)} async-done(((f32[32,3,128]{2,1,0:T(4,128)}), f32[32,3,128]{2,1,0:T(4,128)S(1)}, u32[]{:S(2)}, u32[]{:S(2)}) %all-to-all-start) | async-done | bytes 49184 | tf_op jit(solution)/shard_map/all_to_all | solution.py:440
  263.0 0.6 broadcast_multiply_fusion
  (9 shorter events, 0.1 us)
Async XLA Ops:
  6.5 88.2 %all-gather.3.cloned.1.call-start = ((), (), s32[]{:S(2)}) async-start(), calls=%async_computation.1 | async-start | bytes 9732096 | tf_op jit(solution)/shard_map/all_gather | solution.py:363
  11.9 84.8 %copy-start = (f32[6,8]{1,0:T(8,128)}, f32[6,8]{1,0:T(8,128)S(1)}, u32[]{:S(2)}) copy-start(f32[6,8]{1,0:T(8,128)S(1)} %scatter.4.refs_0_) | copy-start | bytes 580
  201.2 54.2 %copy-start.1 = (f32[128]{0:T(128)S(1)}, f32[128]{0:T(128)}, u32[]{:S(2)}) copy-start(f32[128]{0:T(128)} %param.19) | copy-start | bytes 1540
  252.3 10.7 %all-to-all-start = ((f32[32,3,128]{2,1,0:T(4,128)}), f32[32,3,128]{2,1,0:T(4,128)S(1)}, u32[]{:S(2)}, u32[]{:S(2)}) async-start(f32[32,3,128]{2,1,0:T(4,128)} %forces.1), calls=%async_computation | async-start | bytes 131072 | tf_op jit(solution)/shard_map/all_to_all | solution.py:440
Sparse Core Ops, SparseCore 0:
  10.5 84.2 all-gather.2
